TPU v7x, 768 devices: a whole 4x8x12 slice. The times are simulated.
768 devices in a mesh: ctx: 48 (over y, z_lo), head: 16 (over z_hi, x, core).
Axes of the slice: x: 4, y: 8, z: 12 (z_hi: 2, z_lo: 6; z = z_hi * 6 + z_lo), core: 2. Of those that a mesh axis runs over, the one named last changes fastest.
Arguments:
- queries: bfloat16 [12288, 8192], P('ctx', 'head'), may hold values from -15 to 15
- keys: bfloat16 [12288, 1024], P('ctx'), may hold values from -6 to 6
- values: bfloat16 [12288, 1024], P('ctx'), may hold values from -6 to 6
Outputs:
- attended: bfloat16 [12288, 8192], P('ctx', 'head')
All inputs are finite; a program needn't handle non-finite values.
Results may differ from a plain program's by a relative error of at most 0.015.
Values may be sent and summed in bfloat16 or wider, within the bound.
A program may use at most 128 MiB of HBM per device.

v0:
```python
import jax
import jax.numpy as jnp
from jax import lax
from jax.sharding import PartitionSpec as P

H = 64
KVH = 8
HD = 128


negative_big = -1e30


def side_by_side(arrays, axis, dim, along):
    ends, at = ([], 0)
    for a in arrays[:-1]:
        at += a.shape[along]
        ends.append(at)
    both = jnp.concatenate(arrays, axis=along)
    return tuple(jnp.split(lax.all_gather(both, axis, axis=dim, tiled=True), ends, axis=along))


def attend(acc_state, grouped, key_piece, value_piece, allowed):
    maxima, totals, running_sum = acc_state
    scores = jnp.einsum(
        "qgrd,kgd->grqk", grouped, key_piece, preferred_element_type=jnp.float32
    ) * HD ** (-0.5)
    scores = jnp.where(allowed, scores, negative_big)
    new_max = jnp.maximum(maxima, jnp.max(scores, axis=-1))
    weights = jnp.where(allowed, jnp.exp(scores - new_max[..., None]), 0.0)
    totals = jnp.sum(weights, axis=-1)
    running_sum = jnp.einsum(
        "grqk,kgd->grqd",
        weights.astype(jnp.bfloat16),
        value_piece,
        preferred_element_type=jnp.float32,
    )
    return (new_max, totals, running_sum)


def keep_state(carried):
    return carried


def body(queries, keys, values):
    tok_rows = queries.shape[0]
    heads_dev = queries.shape[1] // HD
    group_size = H // KVH
    kv_count = max(1, heads_dev // group_size)
    repeat = heads_dev // kv_count
    grouped = queries.reshape(tok_rows, kv_count, repeat, HD)
    first_col = lax.axis_index("head") * heads_dev // group_size * HD
    keys_flat = lax.dynamic_slice_in_dim(keys, first_col, kv_count * HD, 1)
    values_flat = lax.dynamic_slice_in_dim(values, first_col, kv_count * HD, 1)
    keys_used = keys_flat.reshape(tok_rows, kv_count, HD)
    values_used = values_flat.reshape(tok_rows, kv_count, HD)
    ctx_place = lax.axis_index("ctx")
    positions = jnp.arange(tok_rows, dtype=jnp.int32)
    blank_state = (
        jnp.full((kv_count, repeat, tok_rows), negative_big, jnp.float32),
        jnp.zeros((kv_count, repeat, tok_rows), jnp.float32),
        jnp.zeros((kv_count, repeat, tok_rows, HD), jnp.float32),
    )
    own_start = ctx_place * tok_rows
    key_piece, value_piece = side_by_side((keys_used, values_used), "ctx", 0, 1)
    key_pos = jnp.arange(key_piece.shape[0], dtype=jnp.int32)
    allowed = (own_start + positions)[:, None] >= key_pos[None, :]
    acc_state = lax.cond(
        jnp.int32(0) <= own_start + tok_rows - 1,
        lambda held: attend(held, grouped, key_piece, value_piece, allowed),
        keep_state,
        blank_state,
    )
    result = acc_state[2] / acc_state[1][..., None]
    return (
        jnp.transpose(result, (2, 0, 1, 3)).reshape(tok_rows, heads_dev * HD).astype(jnp.bfloat16)
    )


def solution(mesh):
    return jax.shard_map(
        body,
        mesh=mesh,
        in_specs=(P("ctx", "head"), P("ctx", None), P("ctx", None)),
        out_specs=P("ctx", "head"),
        check_vma=False,
    )
```

profile of v0, /device:TPU:6, one launch (start us, length us, event | category | flops | bytes accessed | tf_op | source)
XLA Modules:
  0.0 403.4 jit_solution(11075057722848420912)
XLA Ops:
  6.5 0.0 all-gather.2.cloned.1.call-start
  6.5 0.9 dynamic-slice_bitcast_fusion
  7.4 0.7 pad_maximum_fusion
  8.1 0.0 all-gather.2.cloned.1.call-update
  8.1 318.4 %all-gather.2.cloned.1.call-done = bf16[12288,2,128]{2,0,1:T(8,128)(2,1)} async-done(((bf16[256,2,128]{2,0,1:T(8,128)(2,1)}), bf16[12288,2,128]{2,0,1:T(8,128)(2,1)}) %all-gather.2.cloned.1.call-update) | async-done | bytes 6291472 | tf_op jit(solution)/shard_map/all_gather | solution.py:20
  326.5 0.9 ge.18
  327.4 68.1 %conditional.1 = (f32[1,4,256]{2,1,0:T(4,128)S(1)}, f32[1,4,256,128]{3,2,1,0:T(8,128)S(1)}) conditional(s32[]{:T(128)} %convert_element_type.15, () %tuple.13, (s32[]{:T(128)}, s32[256,1]{0,1:T(1,128)S(1)}, s32[256,12288]{0,1:T(8,128)S(1)}, bf16[12288,2,128]{2,0,1:T(8,128)(2,1)}, bf16[256,512]{1,0:T(8,128)(2,1)}) %tuple.14), branch_computations={%region_0.1_spmd, %region_1.4_spmd} | conditional | flops 6609173504 | bytes 183266320 | solution.py:68
  327.4 1.7 broadcast_compare_fusion
  329.1 20.0 %fusion = (f32[4,256]{1,0:T(4,128)S(1)}, f32[12288,256,4]{1,0,2:T(8,128)}) fusion(pred[256,12288]{0,1:T(8,128)(4,1)S(1)} %broadcast_compare_fusion, bf16[12288,2,128]{2,0,1:T(8,128)(2,1)} %get-tuple-element.27, bf16[256,512]{1,0:T(8,128)(2,1)} %get-tuple-element.34), kind=kOutput, calls=%fused_computation.2 | convolution fusion | flops 3258973184 | bytes 56889344 | tf_op jit(solution)/shard_map/cond/branch_1_fun/qgrd,kgd->grqk/dot_general | solution.py:25
  349.1 24.4 %fusion.12 = f32[1,4,256,128]{3,2,1,0:T(8,128)S(1)} fusion(bf16[12288,2,128]{2,0,1:T(8,128)(2,1)} %get-tuple-element.27, f32[12288,256,4]{1,0,2:T(8,128)} %get-tuple-element.36, f32[4,256]{1,0:T(4,128)S(1)} %broadcast_maximum_fusion, pred[256,12288]{0,1:T(8,128)(4,1)S(1)} %broadcast_compare_fusion), kind=kOutput, calls=%fused_computation.14 | convolution fusion | flops 3284140032 | bytes 57151488 | tf_op jit(solution)/shard_map/cond/branch_1_fun/grqk,kgd->grqd/dot_general | solution.py:32
  373.5 21.9 %fusion.2 = f32[4,256]{1,0:T(4,128)S(1)} fusion(f32[12288,256,4]{1,0,2:T(8,128)} %get-tuple-element.36, f32[4,256]{1,0:T(4,128)S(1)} %broadcast_maximum_fusion, pred[256,12288]{0,1:T(8,128)(4,1)S(1)} %broadcast_compare_fusion), kind=kLoop, calls=%fused_computation.4 | loop fusion | flops 62913536 | bytes 53485568 | tf_op jit(solution)/shard_map/cond/branch_1_fun/reduce_sum | solution.py:31
  395.4 0.2 fusion.22
  395.6 0.2 copy.7
  395.9 0.7 copy.18
  (3 shorter events, 0.0 us)
Async XLA Ops:
  6.5 320.0 %all-gather.2.cloned.1.call-start = ((), (), s32[]{:S(2)}) async-start(), calls=%async_computation | async-start | bytes 6422528 | tf_op jit(solution)/shard_map/all_gather | solution.py:20
Sparse Core Ops, SparseCore 0:
  9.7 316.7 all-gather.1
where the time goes:
time: 404 us; the launch traced here: 403 us
  waiting for transfers between devices  318 us (79%)
  matrix products  44.4 us (11%)
  other arithmetic  24.5 us (6%)
  between operations  13.4 us (3%)
    all_gather x1, waiting for transfers between devices, side_by_side(): lax.all_gather(both, axis, axis=dim, tiled=True)  318 us
    dot_general x1, matrix products, attend(): jnp.einsum('grqk,kgd->grqd', weights.astype(jnp.bfloat16), value_piece, p...  24.4 us
    reduce_sum x1, other arithmetic, attend(): totals = jnp.sum(weights, axis=-1)  21.9 us
    dot_general x1, matrix products, attend(): jnp.einsum('qgrd,kgd->grqk', grouped, key_piece, preferred_element_type=j...  20 us
  transfers between devices with their start and end apart: 1, of which 1 were waited for; matrix products, arithmetic and copies ran while one was open for 0% of the time, Pallas kernels for 0%

commit v1 on v0

v1 whole, which is shorter than its diff:
```python
import functools
import jax
import jax.numpy as jnp
from jax import lax
from jax.experimental import pallas as pl
from jax.experimental.pallas import tpu as pltpu
from jax.sharding import PartitionSpec as P

H = 64
KVH = 8
HD = 128

NY = 8
NZ = 6
NX = 4
NH = 2

NEG = -1e30
LOG2E = 1.4426950408889634
MESH = pl.DeviceIdType.MESH


def kernel(q_hbm, k_hbm, v_hbm, o_ref, kv, stage, q_buf, qt, m_ref, l_ref, acc_ref,
           ld_sem, z_send, ring_send, sib_send, ici_recv, sib_recv, *, dims):
    ny, nz, nx = dims
    tok = q_hbm.shape[0]
    heads = q_hbm.shape[1] // HD
    half_z = nz // 2
    full = ny // 2
    span = half_z * tok

    ctx = lax.axis_index("ctx")
    head = lax.axis_index("head")
    y = ctx // nz
    zlo = ctx % nz
    core = head % 2
    x = (head // 2) % nx
    zhi = head // (2 * nx)
    z = zhi * nz + zlo
    ring_z = NH * nz

    def at_y(step):
        return {"ctx": lax.rem(y + step + ny, ny) * nz + zlo, "head": head}

    def at_z(step):
        there = lax.rem(z + step + ring_z, ring_z)
        hi = there // nz
        return {"ctx": y * nz + there % nz, "head": (hi * nx + x) * 2 + core}, hi

    sibling = {"ctx": ctx, "head": head + 1 - 2 * core}

    def columns(ref, g):
        return ref.at[:, pl.ds(pl.multiple_of(g * HD, HD), HD)]

    def chunk(kind, row, col):
        return kv.at[kind, row, pl.ds(pl.multiple_of(col * tok, tok), tok), :]

    g_own = zhi * nx + x

    @pl.when(core == 0)
    def _():
        for hi in range(NH):
            pltpu.make_async_copy(columns(k_hbm, hi * nx + x), stage.at[hi], ld_sem.at[hi]).start()

    @pl.when(core == 1)
    def _():
        for hi in range(NH):
            pltpu.make_async_copy(columns(v_hbm, hi * nx + x), stage.at[hi], ld_sem.at[hi]).start()

    own_k = pltpu.make_async_copy(columns(k_hbm, g_own), chunk(0, y, zlo), ld_sem.at[2])
    own_v = pltpu.make_async_copy(columns(v_hbm, g_own), chunk(1, y, zlo), ld_sem.at[3])
    own_q = pltpu.make_async_copy(q_hbm, q_buf, ld_sem.at[4])
    own_k.start()
    own_v.start()
    own_q.start()

    barrier = pltpu.get_barrier_semaphore()
    peers = [at_y(1), at_y(-1), sibling]
    for d in range(1, half_z + 1):
        peers.append(at_z(d)[0])
        peers.append(at_z(-d)[0])
    for peer in peers:
        pl.semaphore_signal(barrier, inc=1, device_id=peer, device_id_type=MESH)
    for hi in range(NH):
        pltpu.make_async_copy(stage.at[hi], stage.at[hi], ld_sem.at[hi]).wait()
    own_k.wait()
    own_v.wait()
    pl.semaphore_wait(barrier, len(peers))

    def ring_copy(row, col, way, step):
        return pltpu.make_async_remote_copy(
            src_ref=chunk(core, row, col), dst_ref=chunk(core, row, col),
            send_sem=ring_send.at[way, step, col], recv_sem=ici_recv.at[row, col],
            device_id=at_y(1 - 2 * way), device_id_type=MESH)

    def sib_copy(kind, row, col):
        return pltpu.make_async_remote_copy(
            src_ref=chunk(kind, row, col), dst_ref=chunk(kind, row, col),
            send_sem=sib_send.at[row, col], recv_sem=sib_recv.at[row, col],
            device_id=sibling, device_id_type=MESH)

    ring_copy(y, zlo, 0, 0).start()
    ring_copy(y, zlo, 1, 0).start()
    middle = half_z * (1 - 2 * core)
    steps_z = []
    for d in range(1, half_z):
        steps_z += [d, -d]
    steps_z.append(middle)
    z_copies = []
    for n, d in enumerate(steps_z):
        there, hi = at_z(d)
        z_copies.append(pltpu.make_async_remote_copy(
            src_ref=stage.at[hi], dst_ref=chunk(core, y, zlo),
            send_sem=z_send.at[n], recv_sem=ici_recv.at[y, zlo],
            device_id=there, device_id_type=MESH))
        z_copies[-1].start()

    own_q.wait()
    for h in range(heads):
        qt[h] = q_buf[:, h * HD:(h + 1) * HD].astype(jnp.float32).T.astype(jnp.bfloat16)
    m_ref[...] = jnp.full_like(m_ref, NEG)
    l_ref[...] = jnp.zeros_like(l_ref)
    acc_ref[...] = jnp.zeros_like(acc_ref)

    for d in steps_z:
        col = lax.rem(zlo - d + ring_z, nz)
        ring_copy(y, col, 0, 0).wait_recv()
        ring_copy(y, col, 0, 0).start()
        ring_copy(y, col, 1, 0).start()
        sib_copy(core, y, col).start()

    def where_is(item):
        i = jnp.maximum(item - 2, 0)
        step = jnp.where(item < 2, 0, 1 + i // 4)
        way = i % 2
        hf = jnp.where(item < 2, item, jnp.where(step == full, way, (i // 2) % 2))
        row = lax.rem(y + step * (2 * way - 1) + ny, ny)
        return step, way, hf, row

    def move(item):
        step, way, hf, row = where_is(item)
        onward = (step < full - 1) | ((step == full - 1) & (hf == way))
        for jj in range(half_z):
            col = hf * half_z + jj
            ring_copy(row, col, way, step).wait_recv()

            @pl.when(onward)
            def _():
                ring_copy(row, col, way, step).start()
            sib_copy(core, row, col).start()

    def attend(row, hf, masked):
        keys = kv[0, row, pl.ds(pl.multiple_of(hf * span, span), span), :]
        vals_t = kv[1, row, pl.ds(pl.multiple_of(hf * span, span), span), :].T
        scale = LOG2E * HD ** -0.5
        if masked:
            ahead = (lax.broadcasted_iota(jnp.int32, (span, tok), 0)
                     - lax.broadcasted_iota(jnp.int32, (span, tok), 1))
            allowed = ahead <= ctx * tok - (row * nz + hf * half_z) * tok

        def scores(h):
            s = jnp.dot(keys, qt[h], preferred_element_type=jnp.float32)
            return jnp.where(allowed, s, NEG) if masked else s

        s = scores(0)
        for h in range(heads):
            s_next = scores(h + 1) if h + 1 < heads else None
            old = m_ref[h]
            new = jnp.maximum(old, jnp.max(s, axis=0, keepdims=True))
            shrink = jnp.exp2((old - new) * scale)
            w = jnp.exp2((s - new) * scale)
            m_ref[h] = new
            l_ref[h] = l_ref[h] * shrink + jnp.sum(w, axis=0, keepdims=True)
            acc_ref[h] = acc_ref[h] * shrink + jnp.dot(
                vals_t, w.astype(jnp.bfloat16), preferred_element_type=jnp.float32)
            s = s_next

    n_items = 2 + 4 * (full - 1) + 2

    @pl.loop(1, n_items + 1)
    def _(it):
        @pl.when((it >= 2) & (it < n_items))
        def _():
            move(it)
        item = it - 1
        step, way, hf, row = where_is(item)
        for jj in range(half_z):
            col = hf * half_z + jj

            @pl.when((item >= 2) | (col != zlo))
            def _():
                sib_copy(1 - core, row, col).wait_recv()

        @pl.when((item < 2) & (hf * half_z <= zlo))
        def _():
            attend(row, hf, True)

        @pl.when((item >= 2) & (row < y))
        def _():
            attend(row, hf, False)

    for h in range(heads):
        out = (acc_ref[h] / l_ref[h]).T
        o_ref[:, h * HD:(h + 1) * HD] = out.astype(jnp.bfloat16)

    for copy in z_copies:
        copy.wait_send()

    @pl.loop(0, nz)
    def _(col):
        for way in range(2):
            for step in range(full - 1):
                ring_copy(y, col, way, step).wait_send()
            @pl.when((col // half_z) == way)
            def _():
                ring_copy(y, col, way, full - 1).wait_send()

    @pl.loop(0, ny)
    def _(row):
        @pl.loop(0, nz)
        def _(col):
            @pl.when((row != y) | (col != zlo))
            def _():
                sib_copy(core, row, col).wait_send()


def attention(queries, keys, values, dims):
    ny, nz, nx = dims
    tok = queries.shape[0]
    heads = queries.shape[1] // HD
    any_space = pl.BlockSpec(memory_space=pl.ANY)
    dma = pltpu.SemaphoreType.DMA
    return pl.pallas_call(
        functools.partial(kernel, dims=dims),
        out_shape=jax.ShapeDtypeStruct(queries.shape, jnp.bfloat16),
        in_specs=[any_space] * 3,
        out_specs=pl.BlockSpec(memory_space=pltpu.VMEM),
        scratch_shapes=[
            pltpu.VMEM((2, ny, nz * tok, HD), jnp.bfloat16),
            pltpu.VMEM((NH, tok, HD), jnp.bfloat16),
            pltpu.VMEM((tok, heads * HD), jnp.bfloat16),
            pltpu.VMEM((heads, HD, tok), jnp.bfloat16),
            pltpu.VMEM((heads, 1, tok), jnp.float32),
            pltpu.VMEM((heads, 1, tok), jnp.float32),
            pltpu.VMEM((heads, HD, tok), jnp.float32),
            dma((5,)),
            dma((nz - 1,)),
            dma((2, ny // 2, nz)),
            dma((ny, nz)),
            dma((ny, nz)),
            dma((ny, nz)),
        ],
        compiler_params=pltpu.CompilerParams(
            collective_id=0, has_side_effects=True, vmem_limit_bytes=48 * 1024 * 1024),
        name="causal_ring",
    )(queries, keys, values)


def solution(mesh):
    return jax.shard_map(
        functools.partial(attention, dims=(NY, NZ, NX)),
        mesh=mesh,
        in_specs=(P("ctx", "head"), P("ctx", None), P("ctx", None)),
        out_specs=P("ctx", "head"),
        check_vma=False,
    )
```

time: 404 us -> 60.7 us (0.15)
  the two profiles are of different devices: /device:TPU:6 before, /device:TPU:35 now
where the time goes in v1:
time: 60.7 us; the launch traced here: 60.4 us
  Pallas kernels  56.7 us (93%)
  local copies, waits for them, and re-layouts  3.74 us (6%)
    pallas_call x1, Pallas kernels, attention(): pl.pallas_call(functools.partial(kernel, dims=dims), out_shape=jax.ShapeD...  56.7 us
    unnamed x7, local copies, waits for them, and re-layouts  3.74 us

profile of v1, /device:TPU:35, one launch (start us, length us, event | category | flops | bytes accessed | tf_op | source)
XLA Modules:
  0.0 60.4 jit_solution(7097399094879863785)
XLA Ops:
  0.0 0.0 copy-start
  0.0 1.0 %copy-done = bf16[256,1024]{1,0:T(8,128)(2,1)S(1)} copy-done((bf16[256,1024]{1,0:T(8,128)(2,1)S(1)}, bf16[256,1024]{1,0:T(8,128)(2,1)}, u32[]{:S(2)}) %copy-start) | copy-done | bytes 524312
  1.0 0.0 copy-start.1
  1.0 1.0 %copy-done.1 = bf16[256,1024]{1,0:T(8,128)(2,1)S(1)} copy-done((bf16[256,1024]{1,0:T(8,128)(2,1)S(1)}, bf16[256,1024]{1,0:T(8,128)(2,1)}, u32[]{:S(2)}) %copy-start.1) | copy-done | bytes 524312
  2.1 0.0 copy-start.2
  2.1 0.9 %copy-done.2 = bf16[256,512]{1,0:T(8,128)(2,1)S(1)} copy-done((bf16[256,512]{1,0:T(8,128)(2,1)S(1)}, bf16[256,512]{1,0:T(8,128)(2,1)}, u32[]{:S(2)}) %copy-start.2) | copy-done | bytes 262168
  3.0 56.7 %causal_ring.1 = bf16[256,512]{1,0:T(8,128)(2,1)S(1)} custom-call(bf16[256,512]{1,0:T(8,128)(2,1)S(1)} %copy-done.2, bf16[256,1024]{1,0:T(8,128)(2,1)S(1)} %copy-done, bf16[256,1024]{1,0:T(8,128)(2,1)S(1)} %copy-done.1), custom_call_target="tpu_custom_call" | custom-call | tf_op jit(solution)/shard_map/causal_ring/pallas_call | solution.py:233
  59.7 0.7 %copy.5 = bf16[256,512]{1,0:T(8,128)(2,1)} copy(bf16[256,512]{1,0:T(8,128)(2,1)S(1)} %causal_ring.1) | data formatting | bytes 524288
Async XLA Ops:
  0.0 1.0 %copy-start = (bf16[256,1024]{1,0:T(8,128)(2,1)S(1)}, bf16[256,1024]{1,0:T(8,128)(2,1)}, u32[]{:S(2)}) copy-start(bf16[256,1024]{1,0:T(8,128)(2,1)} %k_hbm.1) | copy-start | bytes 1572868
  1.0 1.0 %copy-start.1 = (bf16[256,1024]{1,0:T(8,128)(2,1)S(1)}, bf16[256,1024]{1,0:T(8,128)(2,1)}, u32[]{:S(2)}) copy-start(bf16[256,1024]{1,0:T(8,128)(2,1)} %v_hbm.1) | copy-start | bytes 1572868
  2.1 0.9 %copy-start.2 = (bf16[256,512]{1,0:T(8,128)(2,1)S(1)}, bf16[256,512]{1,0:T(8,128)(2,1)}, u32[]{:S(2)}) copy-start(bf16[256,512]{1,0:T(8,128)(2,1)} %q_hbm.1) | copy-start | bytes 786436
